TPU v7x, 256 devices: a whole 4x4x8 slice. The times are simulated.
256 devices in a mesh: gx: 8 (over x, core), gy: 8 (over z), wa: 4 (over y).
Axes of the slice: x: 4, y: 4, z: 8, core: 2. Of those that a mesh axis runs over, the one named last changes fastest.
Arguments:
- velocity: float32 [3, 256, 512, 512], P(None, 'gx', 'gy', 'wa'), may hold values from -70 to 70, as said below
- lengths: int32 [8, 8, 4, 2048], P('gx', 'gy', 'wa'), may hold values from 16 to 128
- destinations: int32 [8, 8, 4, 2048, 1], P('gx', 'gy', 'wa'), may hold values from 0 to 63; in each aligned block of 2048 rows (0 to 2047, 2048 to 4095, ..., all dimensions but the last counted through in order) at most 64 rows name the same one
Outputs:
- received: float32 [64, 4, 3, 64, 64, 128], P(('gx', 'gy'), 'wa')
Inputs may be any that keep to these rules, and one draw needn't show every extreme that they name: `velocity`: finite values; the amplitude varies over the grid. `destinations`: in every draw no device sends more than 64 blocks to one writer, and some device sends exactly 64 to one writer.
All inputs are finite; a program needn't handle non-finite values.
Results may differ from a plain program's by a relative error of at most 0.0003.
Values sent between devices are 32-bit elements; how exact they have to be, the bound alone decides.
A program may use at most 128 MiB of HBM per device.

v0:
```python
import jax
import jax.numpy as jnp
from jax import lax
from jax.sharding import Mesh
from jax.sharding import PartitionSpec as P

BY = 8
BZ = 16
GX_GY_WA = ("gx_0", "gx_1", "gy", "wa")
GX = ("gx_0", "gx_1")
GX_GY = ("gx_0", "gx_1", "gy")


def extended(array, sides, width):
    for axis, dim in sides:
        peers, length = (lax.axis_size(axis), array.shape[dim])
        up = [(i, (i + 1) % peers) for i in range(peers)]
        down = [(j, i) for i, j in up]
        last = lax.slice_in_dim(array, length - width, length, axis=dim)
        leading = lax.slice_in_dim(array, 0, width, axis=dim)
        before = lax.ppermute(last, axis, up)
        after = lax.ppermute(leading, axis, down)
        array = jnp.concatenate([before, array, after], axis=dim)
    return array


def over_axes(array, axes):
    for axis in axes:
        array = lax.psum(array, axis)
    return array


def dct_table(count):
    freqs = jnp.arange(count, dtype=jnp.float32)[:, None]
    points = jnp.arange(count, dtype=jnp.float32)[None, :]
    table = jnp.cos(jnp.pi * (points + 0.5) * freqs / count) * jnp.sqrt(2.0 / count)
    return jnp.where(freqs == 0.0, table * jnp.sqrt(0.5), table)


def curl_field(padded):

    def along_x(component):
        return (padded[component, 2:, 1:-1, 1:-1] - padded[component, :-2, 1:-1, 1:-1]) * 0.5

    def along_y(component):
        return (padded[component, 1:-1, 2:, 1:-1] - padded[component, 1:-1, :-2, 1:-1]) * 0.5

    def along_z(component):
        return (padded[component, 1:-1, 1:-1, 2:] - padded[component, 1:-1, 1:-1, :-2]) * 0.5

    first = along_y(2) - along_z(1)
    second = along_z(0) - along_x(2)
    third = along_x(1) - along_y(0)
    return jnp.stack([first, second, third])


def transform(curl):
    comps, cells_x, cells_y, cells_z = curl.shape
    kron_table = jnp.kron(dct_table(BY), dct_table(BZ)).T.reshape(BY, BZ, BY * BZ)
    grouped = curl.reshape(comps, cells_x, cells_y // BY, BY, cells_z // BZ, BZ)
    coeffs = lax.dot_general(
        grouped,
        kron_table,
        (((3, 5), (0, 1)), ((), ())),
        precision=lax.Precision.HIGHEST,
        preferred_element_type=jnp.float32,
    )
    return coeffs.reshape(comps, -1, BY * BZ)


def local(velocity, lengths, destinations):
    padded = extended(velocity, ((GX, 1), ("gy", 2), ("wa", 3)), 1)
    curl = curl_field(padded)
    coeffs = transform(curl)
    total = over_axes(jnp.sum(coeffs * coeffs), GX_GY_WA)
    every = curl.size * lax.axis_size(GX) * lax.axis_size("gy") * lax.axis_size("wa")
    rms = jnp.sqrt(total / every + 1e-06)
    comps, nblk, width = coeffs.shape
    rows_x = lax.axis_size(GX)
    rows_y = lax.axis_size("gy")
    writer_count = rows_x * rows_y
    capacity = max(2, 2 * nblk // writer_count)
    targets = destinations.reshape(nblk)
    lens = lengths.reshape(nblk)
    onehot = (targets[:, None] == jnp.arange(writer_count, dtype=jnp.int32)[None, :]).astype(
        jnp.int32
    )
    before = jnp.cumsum(onehot, axis=0) - onehot
    ranking = jnp.sum(before * onehot, axis=1)
    slot_index = targets * capacity + ranking
    source = jnp.full((writer_count * capacity,), -1, jnp.int32)
    source = source.at[slot_index].set(jnp.arange(nblk, dtype=jnp.int32))
    present = source >= 0
    safe = jnp.maximum(source, 0)
    picked = jnp.take(coeffs, safe, axis=1)
    freqs = jnp.arange(width, dtype=jnp.int32)
    keep = (freqs[None, :] < jnp.take(lens, safe)[:, None]) & present[:, None]
    outgoing = jnp.where(keep[None, :, :], picked / rms, 0.0)
    outgoing = outgoing.reshape(comps, writer_count, capacity, width)
    arrived = lax.all_to_all(outgoing, GX_GY, split_axis=1, concat_axis=1, tiled=True)
    return arrived.reshape(1, 1, comps, writer_count, capacity, width)


def solution(mesh):
    finer = Mesh(
        mesh.devices.reshape(4, 2, mesh.shape["gy"], mesh.shape["wa"]), ("gx_0", "gx_1", "gy", "wa")
    )
    return jax.shard_map(
        local,
        mesh=finer,
        in_specs=(P(None, GX, "gy", "wa"), P(GX, "gy", "wa", None), P(GX, "gy", "wa", None, None)),
        out_specs=P(GX_GY, "wa", None, None, None, None),
        check_vma=False,
    )
```

profile of v0, /device:TPU:1, one launch (start us, length us, event | category | flops | bytes accessed | tf_op | source)
XLA Modules:
  0.0 446.5 jit_solution(11419711120034385909)
XLA Ops:
  0.0 1.0 fusion.18
  1.0 2.6 collective-permute-start
  3.6 0.6 collective-permute-start.1
  4.3 0.7 fusion.11
  5.0 18.1 %reduce-window.6 = s32[64,16,128]{2,1,0:T(8,128)S(1)} reduce-window(s32[64,16,128]{2,1,0:T(8,128)S(1)} %fusion.11, s32[]{:T(128)} %constant.25.clone.1), window={size=1x1x128 pad=0_0x0_0x127_0}, to_apply=%region_0.1 | reduce-window | flops 16646144 | bytes 1048580 | tf_op jit(solution)/shard_map/reduce-window
  23.1 0.2 slice.96
  23.4 0.4 copy.38
  23.8 0.2 reduce-window.9
  24.0 0.2 broadcast_add_fusion
  24.2 0.3 fusion.10
  24.5 8.1 %scatter_custom_fusion = s32[4096]{0:T(1024)S(1)} fusion(s32[2048]{0:T(1024)S(1)} %bitcast.68, s32[2048]{0:T(1024)S(1)} %iota.50, s32[]{:T(128)} %constant.22.clone.1), kind=kCustom, calls=%fused_computation.48 | custom fusion | bytes 16388 | tf_op jit(solution)/shard_map/scatter | solution.py:92
  32.6 23.0 %gather_fusion = s32[4096]{0:T(1024)S(1)} fusion(s32[2048]{0:T(1024)S(1)} %bitcast.54, s32[4096]{0:T(1024)S(1)} %maximum_clamp_fusion), kind=kCustom, calls=%fused_computation | custom fusion | bytes 49152 | tf_op jit(solution)/shard_map/jit(_take)/gather | solution.py:97
  56.0 2.3 fusion.7
  58.5 0.2 mul.189
  58.7 0.9 constant_dynamic-update-slice_fusion.6
  59.6 2.8 constant_dynamic-update-slice_fusion.5
  62.5 0.9 constant_dynamic-update-slice_fusion.3
  63.4 0.7 fusion.15
  64.1 5.0 %collective-permute-start.2 = (f32[3,34,1,128]{3,2,1,0:T(1,128)}, f32[3,34,1,128]{3,2,1,0:T(1,128)S(1)}, u32[]{:S(2)}, u32[]{:S(2)}) collective-permute-start(f32[3,34,1,128]{3,2,1,0:T(1,128)} %get-tuple-element.18), channel_id=1, source_target_pairs={{4,0},{8,4},{12,8},{16,12},{20,16},{24,20},{28,24},{0,28},{5,1},{9... | collective-permute-start | bytes 156680 | tf_op jit(solution)/shard_map/ppermute | solution.py:22
  69.0 1.5 fusion.17
  70.6 1.5 fusion.16
  72.0 3.6 copy.41
  75.6 3.7 copy.42
  79.3 3.7 copy.43
  83.0 3.8 copy.44
  86.8 2.5 pad_maximum_fusion.2
  89.3 10.2 %copy.23 = f32[3,34,66,128]{1,3,2,0:T(8,128)} copy(f32[3,34,66,128]{3,2,1,0:T(8,128)} %pad_maximum_fusion.2) | data formatting | bytes 6893568 | tf_op jit(solution)/shard_map/concatenate | solution.py:23
  99.4 2.2 fusion.14
  101.7 2.7 collective-permute-start.4
  104.4 2.3 pad_maximum_fusion.5
  106.7 3.8 copy.45
  110.4 2.7 copy.46
  113.1 10.3 %multiply_subtract_fusion = f32[1,32,64,128]{1,3,2,0:T(8,128)} fusion(f32[1,32,64,128]{1,3,2,0:T(8,128)} %copy.45, f32[1,32,64,128]{1,3,2,0:T(8,128)} %copy.46, f32[1,32,64,128]{1,3,2,0:T(8,128)} %copy.43, f32[1,32,64,128]{1,3,2,0:T(8,128)} %copy.44), kind=kLoop, calls=%fused_computation.15 | loop fusion | flops 1310720 | bytes 5242880 | tf_op jit(solution)/shard_map/sub | solution.py:53
  123.4 2.7 copy.39
  126.2 2.8 copy.40
  129.0 18.5 %fusion.6 = (f32[1,32,64,128]{1,3,2,0:T(8,128)}, f32[1,32,64,128]{1,3,2,0:T(8,128)}) fusion(f32[3,34,66,128]{1,3,2,0:T(8,128)} %copy.23, f32[3,34,66,1]{1,3,2,0:T(1,128)} %collective-permute-done.5, f32[3,34,66,1]{1,3,2,0:T(1,128)} %collective-permute-done.4, f32[1,32,64,128]{1,3,2,0:T(8,128)} %copy.39, f32[1,32,64,128]{1,3,2,0:T(8,128)} %copy.40, ...), kind=kLoop, calls=%fused_computation.14 | loop fusion | flops 3670016 | bytes 9792096 | tf_op jit(solution)/shard_map/sub | solution.py:51
  147.5 10.3 %maximum_bitcast_fusion = f32[3,32,8,8,8,16]{1,5,3,4,2,0:T(8,128)} fusion(f32[1,32,8,8,8,16]{1,5,4,3,2,0:T(8,128)S(1)} %bitcast.58, f32[1,32,8,8,8,16]{1,5,4,3,2,0:T(8,128)} %bitcast.60, f32[1,32,8,8,8,16]{1,5,4,3,2,0:T(8,128)} %bitcast.59), kind=kLoop, calls=%fused_computation.3 | loop fusion | flops 1572864 | bytes 6291456 | tf_op jit(solution)/shard_map/dot_general | solution.py:61
  157.8 23.1 %copy.47 = f32[3,32,8,8,8,16]{5,3,2,1,4,0:T(8,128)} copy(f32[3,32,8,8,8,16]{1,5,3,4,2,0:T(8,128)} %maximum_bitcast_fusion) | data formatting | bytes 6291456 | tf_op jit(solution)/shard_map/dot_general | solution.py:61
  180.9 24.0 %multiply_reduce_fusion = (f32[]{:T(128)}, f32[3,2048,128]{2,1,0:T(8,128)S(1)}) fusion(f32[3,2048,8,16]{3,1,2,0:T(8,128)} %bitcast.55, f32[8,16,128,1]{2,1,0,3:T(8,128)S(1)} %bitcast.62), kind=kOutput, calls=%fused_computation.17 | convolution fusion | flops 1209532416 | bytes 6356996 | tf_op jit(solution)/shard_map/dot_general | solution.py:61
  204.9 8.1 %psum.28 = f32[]{:T(128)} all-reduce(f32[]{:T(128)} %get-tuple-element.32), channel_id=1, replica_groups=mesh['gx_0'=4,'gx_1'=2,'gy'=8,'wa'=4] {'gx_0'}, use_global_device_ids=true, to_apply=%region_5.6 | all-reduce | flops 1 | bytes 8 | tf_op jit(solution)/shard_map/psum | solution.py:29
  213.0 7.0 %psum.29 = f32[]{:T(128)} all-reduce(f32[]{:T(128)} %psum.28), channel_id=1, replica_groups=mesh['gx_0'=4,'gx_1'=2,'gy'=8,'wa'=4] {'gx_1'}, use_global_device_ids=true, to_apply=%region_6.7 | all-reduce | flops 1 | bytes 8 | tf_op jit(solution)/shard_map/psum | solution.py:29
  220.0 10.0 %copy.34 = f32[3,2048,128]{2,0,1:T(4,128)} copy(f32[3,2048,128]{2,1,0:T(8,128)S(1)} %get-tuple-element.33) | data formatting | bytes 6291456 | tf_op jit(solution)/shard_map/dot_general | solution.py:61
  229.9 14.2 %psum.30 = f32[]{:T(128)} all-reduce(f32[]{:T(128)} %psum.29), channel_id=1, replica_groups=mesh['gx_0'=4,'gx_1'=2,'gy'=8,'wa'=4] {'gy'}, use_global_device_ids=true, to_apply=%region_7.8 | all-reduce | flops 1 | bytes 8 | tf_op jit(solution)/shard_map/psum | solution.py:29
  244.2 32.5 %gather_fusion.1 = f32[4096,3,128]{2,1,0:T(4,128)} fusion(f32[3,2048,128]{2,0,1:T(4,128)} %copy.34, s32[4096]{0:T(1024)S(1)} %maximum_clamp_fusion), kind=kCustom, calls=%fused_computation.1 | custom fusion | bytes 12599296 | tf_op jit(solution)/shard_map/jit(_take)/gather | solution.py:95
  276.7 9.5 %psum.31 = f32[]{:T(128)} all-reduce(f32[]{:T(128)} %psum.30), channel_id=1, replica_groups=mesh['gx_0'=4,'gx_1'=2,'gy'=8,'wa'=4] {'wa'}, use_global_device_ids=true, to_apply=%region_8.9 | all-reduce | flops 1 | bytes 8 | tf_op jit(solution)/shard_map/psum | solution.py:29
  286.9 5.0 %fusion.1 = f32[3,64,64,128]{3,2,0,1:T(8,128)S(1)} fusion(f32[3,64,64,128]{3,0,2,1:T(4,128)} %bitcast.56, f32[]{:T(128)S(6)} %sqrt.3, pred[64,64]{1,0:T(8,128)(4,1)S(1)} %broadcast_in_dim.69, pred[64,64,128]{2,1,0:T(8,128)(4,1)S(1)} %copy-done.6), kind=kLoop, calls=%fused_computation.6 | loop fusion | flops 4718592 | bytes 13111300 | tf_op jit(solution)/shard_map/jit(_where)/select_n | solution.py:98
  291.9 151.2 %all_to_all.5 = f32[3,64,64,128]{3,2,0,1:T(8,128)S(1)} all-to-all(f32[3,64,64,128]{3,2,0,1:T(8,128)S(1)} %fusion.1), channel_id=1, replica_groups=mesh['gx_0'=4,'gx_1'=2,'gy'=8,'wa'=4] {'gx_0','gx_1','gy'}, dimensions={1} | all-to-all | bytes 12582912 | tf_op jit(solution)/shard_map/all_to_all | solution.py:100
  443.2 3.3 copy.36
  (39 shorter events, 0.7 us)
Async XLA Ops:
  0.0 32.6 %copy-start = (s32[1,1,1,2048]{3,2,1,0:T(1,128)S(1)}, s32[1,1,1,2048]{3,2,1,0:T(1,128)}, u32[]{:S(2)}) copy-start(s32[1,1,1,2048]{3,2,1,0:T(1,128)} %param.4) | copy-start | bytes 24580
  0.0 24.2 %copy-start.7 = (s32[1,1,1,2048,1]{3,4,2,1,0:T(1,128)S(1)}, s32[1,1,1,2048,1]{3,4,2,1,0:T(1,128)}, u32[]{:S(2)}) copy-start(s32[1,1,1,2048,1]{3,4,2,1,0:T(1,128)} %param.5) | copy-start | bytes 24580
  1.0 57.7 %collective-permute-start = (f32[3,1,64,128]{3,2,1,0:T(8,128)S(1)}, f32[3,1,64,128]{3,2,1,0:T(8,128)}, u32[]{:S(2)}, u32[]{:S(2)}) collective-permute-start(f32[3,1,64,128]{3,2,1,0:T(8,128)S(1)} %get-tuple-element.27), channel_id=1, source_target_pairs={{0,32},{32,64},{64,96},{96,128},{128,160},{160,192},{192,224},{224... | collective-permute-start | bytes 294920 | tf_op jit(solution)/shard_map/ppermute | solution.py:21
  3.6 58.9 %collective-permute-start.1 = (f32[3,1,64,128]{3,2,1,0:T(8,128)S(1)}, f32[3,1,64,128]{3,2,1,0:T(8,128)}, u32[]{:S(2)}, u32[]{:S(2)}) collective-permute-start(f32[3,1,64,128]{3,2,1,0:T(8,128)S(1)} %get-tuple-element.26), channel_id=1, source_target_pairs={{32,0},{64,32},{96,64},{128,96},{160,128},{192,160},{224,192},{0,2... | collective-permute-start | bytes 294920 | tf_op jit(solution)/shard_map/ppermute | solution.py:22
  64.1 22.7 %collective-permute-start.2 = (f32[3,34,1,128]{3,2,1,0:T(1,128)}, f32[3,34,1,128]{3,2,1,0:T(1,128)S(1)}, u32[]{:S(2)}, u32[]{:S(2)}) collective-permute-start(f32[3,34,1,128]{3,2,1,0:T(1,128)} %get-tuple-element.18), channel_id=1, source_target_pairs={{4,0},{8,4},{12,8},{16,12},{20,16},{24,20},{28,24},{0,28},{5,1},{9... | collective-permute-start | bytes 156680 | tf_op jit(solution)/shard_map/ppermute | solution.py:22
  69.0 17.8 %collective-permute-start.3 = (f32[3,34,1,128]{3,2,1,0:T(1,128)}, f32[3,34,1,128]{3,2,1,0:T(1,128)S(1)}, u32[]{:S(2)}, u32[]{:S(2)}) collective-permute-start(f32[3,34,1,128]{3,2,1,0:T(1,128)} %get-tuple-element.17), channel_id=1, source_target_pairs={{0,4},{4,8},{8,12},{12,16},{16,20},{20,24},{24,28},{28,0},{1,5},{5... | collective-permute-start | bytes 156680 | tf_op jit(solution)/shard_map/ppermute | solution.py:21
  101.7 27.3 %collective-permute-start.4 = (f32[3,34,66,1]{1,3,2,0:T(1,128)}, f32[3,34,66,1]{1,3,2,0:T(1,128)}, u32[]{:S(2)}, u32[]{:S(2)}) collective-permute-start(f32[3,34,66,1]{1,3,2,0:T(1,128)} %get-tuple-element.9), channel_id=1, source_target_pairs={{1,0},{2,1},{3,2},{0,3},{5,4},{6,5},{7,6},{4,7},{9,8},{10,9},{11,1... | collective-permute-start | bytes 80792 | tf_op jit(solution)/shard_map/ppermute | solution.py:22
  104.4 24.6 %collective-permute-start.5 = (f32[3,34,66,1]{1,3,2,0:T(1,128)}, f32[3,34,66,1]{1,3,2,0:T(1,128)}, u32[]{:S(2)}, u32[]{:S(2)}) collective-permute-start(f32[3,34,66,1]{1,3,2,0:T(1,128)} %get-tuple-element.10), channel_id=1, source_target_pairs={{0,1},{1,2},{2,3},{3,0},{4,5},{5,6},{6,7},{7,4},{8,9},{9,10},{10,1... | collective-permute-start | bytes 80792 | tf_op jit(solution)/shard_map/ppermute | solution.py:21
  106.7 3.8 copy-start.5
  113.1 10.3 %copy-start.4 = (f32[1,32,64,128]{3,2,1,0:T(8,128)S(1)}, f32[1,32,64,128]{3,2,1,0:T(8,128)}, u32[]{:S(2)}) copy-start(f32[1,32,64,128]{3,2,1,0:T(8,128)} %get-tuple-element.16) | copy-start | bytes 3145732
  123.4 2.7 copy-start.3
  129.0 18.5 %copy-start.2 = (f32[1,32,64,128]{1,3,2,0:T(8,128)S(1)}, f32[1,32,64,128]{1,3,2,0:T(8,128)}, u32[]{:S(2)}) copy-start(f32[1,32,64,128]{1,3,2,0:T(8,128)} %multiply_subtract_fusion) | copy-start | bytes 3145732
  244.2 42.7 %copy-start.6 = (pred[64,64,128]{2,1,0:T(8,128)(4,1)S(1)}, pred[64,64,128]{2,1,0:T(8,128)(4,1)}, u32[]{:S(2)}) copy-start(pred[64,64,128]{2,1,0:T(8,128)(4,1)} %fusion.7) | copy-start | bytes 1572868
  443.2 3.3 copy-start.1
where the time goes:
time: 448 us; the launch traced here: 446 us
  blocking collectives  190 us (42%)
  local copies, waits for them, and re-layouts  149 us (33%)
  other arithmetic  71.2 us (16%)
  matrix products  24 us (5%)
  starting transfers between devices  10.9 us (2%)
    all_to_all x1, blocking collectives, local(): lax.all_to_all(outgoing, GX_GY, split_axis=1, concat_axis=1, tiled=True)  151 us
    psum x4, blocking collectives, over_axes(): array = lax.psum(array, axis)  38.8 us
    dot_general x2, local copies, waits for them, and re-layouts, transform(): lax.dot_general(grouped, kron_table, (((3, 5), (0, 1)), ((), ())), precis...  33 us
    gather x1, local copies, waits for them, and re-layouts, local(): picked = jnp.take(coeffs, safe, axis=1)  32.5 us
    unnamed x25, local copies, waits for them, and re-layouts  27.7 us
    dot_general x1, matrix products, transform(): lax.dot_general(grouped, kron_table, (((3, 5), (0, 1)), ((), ())), precis...  24 us
    gather x1, local copies, waits for them, and re-layouts, local(): keep = (freqs[None, :] < jnp.take(lens, safe)[:, None]) & present[:, None]  23 us
    another operation x3, other arithmetic  18.5 us
  transfers between devices with their start and end apart: 6, of which 0 were waited for; matrix products, arithmetic and copies ran while one was open for 22% of the time, Pallas kernels for 0%

commit v1 on v0

--- a/solution.py
+++ b/solution.py
@@ -26,7 +26,7 @@
 
 def over_axes(array, axes):
     for axis in axes:
-        array = lax.psum(array, axis)
+        array = jnp.sum(lax.all_gather(array, axis), axis=0)
     return array
 
 

time: 448 us -> 465 us (1.038); the launches traced: 446 us -> 456 us
  local copies, waits for them, and re-layouts: 149 us -> 158 us
    psum x4 -> x0, blocking collectives: 38.8 us -> none  [over_axes(): array = lax.psum(array, axis)]
    unnamed x0 -> x4, blocking collectives: none -> 36.5 us
    unnamed x25 -> x44, local copies, waits for them, and re-layouts: 27.7 us -> 35.9 us
where the time goes in v1:
time: 465 us; the launch traced here: 456 us
  blocking collectives  188 us (40%)
  local copies, waits for them, and re-layouts  158 us (34%)
  other arithmetic  73.7 us (16%)
  matrix products  24.2 us (5%)
  starting transfers between devices  11.4 us (2%)
    all_to_all x1, blocking collectives, local(): lax.all_to_all(outgoing, GX_GY, split_axis=1, concat_axis=1, tiled=True)  151 us
    unnamed x4, blocking collectives  36.5 us
    unnamed x44, local copies, waits for them, and re-layouts  35.9 us
    dot_general x2, local copies, waits for them, and re-layouts, transform(): lax.dot_general(grouped, kron_table, (((3, 5), (0, 1)), ((), ())), precis...  33 us
    gather x1, local copies, waits for them, and re-layouts, local(): picked = jnp.take(coeffs, safe, axis=1)  32.5 us
    dot_general x1, matrix products, transform(): lax.dot_general(grouped, kron_table, (((3, 5), (0, 1)), ((), ())), precis...  24.2 us
    gather x1, local copies, waits for them, and re-layouts, local(): keep = (freqs[None, :] < jnp.take(lens, safe)[:, None]) & present[:, None]  23 us
    sub x1, other arithmetic, curl_field(): first = along_y(2) - along_z(1)  18.6 us
  transfers between devices with their start and end apart: 6, of which 0 were waited for; matrix products, arithmetic and copies ran while one was open for 22% of the time, Pallas kernels for 0%

profile of v1, /device:TPU:1, one launch (start us, length us, event | category | flops | bytes accessed | tf_op | source)
XLA Modules:
  0.0 455.8 jit_solution(15672844000622357451)
XLA Ops:
  0.0 1.0 fusion.18
  1.0 2.6 collective-permute-start
  4.3 0.7 fusion.11
  5.0 18.1 %reduce-window.6 = s32[64,16,128]{2,1,0:T(8,128)S(1)} reduce-window(s32[64,16,128]{2,1,0:T(8,128)S(1)} %fusion.11, s32[]{:T(128)} %constant.25.clone.1), window={size=1x1x128 pad=0_0x0_0x127_0}, to_apply=%region_0.1 | reduce-window | flops 16646144 | bytes 1048580 | tf_op jit(solution)/shard_map/reduce-window
  24.5 8.1 %scatter_custom_fusion = s32[4096]{0:T(1024)S(1)} fusion(s32[2048]{0:T(1024)S(1)} %bitcast.76, s32[2048]{0:T(1024)S(1)} %iota.50, s32[]{:T(128)} %constant.22.clone.1), kind=kCustom, calls=%fused_computation.48 | custom fusion | bytes 16388 | tf_op jit(solution)/shard_map/scatter | solution.py:92
  32.6 23.0 %gather_fusion = s32[4096]{0:T(1024)S(1)} fusion(s32[2048]{0:T(1024)S(1)} %bitcast.62, s32[4096]{0:T(1024)S(1)} %maximum_clamp_fusion), kind=kCustom, calls=%fused_computation | custom fusion | bytes 49152 | tf_op jit(solution)/shard_map/jit(_take)/gather | solution.py:97
  56.1 2.4 fusion.7
  58.8 0.7 dynamic-slice
  59.4 0.7 dynamic-slice.1
  60.7 0.9 constant_dynamic-update-slice_fusion.6
  61.6 2.8 constant_dynamic-update-slice_fusion.5
  64.4 0.9 constant_dynamic-update-slice_fusion.3
  65.3 0.7 fusion.15
  66.0 5.0 %collective-permute-start.2 = (f32[3,34,1,128]{3,2,1,0:T(1,128)}, f32[3,34,1,128]{3,2,1,0:T(1,128)S(1)}, u32[]{:S(2)}, u32[]{:S(2)}) collective-permute-start(f32[3,34,1,128]{3,2,1,0:T(1,128)} %get-tuple-element.18), channel_id=1, source_target_pairs={{4,0},{8,4},{12,8},{16,12},{20,16},{24,20},{28,24},{0,28},{5,1},{9... | collective-permute-start | bytes 156680 | tf_op jit(solution)/shard_map/ppermute | solution.py:22
  71.0 1.5 fusion.17
  72.5 1.5 fusion.16
  74.0 3.6 copy.41
  77.6 3.7 copy.42
  81.3 3.7 copy.43
  85.0 3.8 copy.44
  88.8 2.5 pad_maximum_fusion.2
  91.3 10.2 %copy.23 = f32[3,34,66,128]{1,3,2,0:T(8,128)} copy(f32[3,34,66,128]{3,2,1,0:T(8,128)} %pad_maximum_fusion.2) | data formatting | bytes 6893568 | tf_op jit(solution)/shard_map/concatenate | solution.py:23
  101.5 2.2 fusion.14
  103.7 2.7 collective-permute-start.4
  106.9 2.3 pad_maximum_fusion.5
  109.1 3.8 copy.45
  112.9 2.7 copy.46
  115.6 10.3 %multiply_subtract_fusion = f32[1,32,64,128]{1,3,2,0:T(8,128)} fusion(f32[1,32,64,128]{1,3,2,0:T(8,128)} %copy.45, f32[1,32,64,128]{1,3,2,0:T(8,128)} %copy.46, f32[1,32,64,128]{1,3,2,0:T(8,128)} %copy.43, f32[1,32,64,128]{1,3,2,0:T(8,128)} %copy.44), kind=kLoop, calls=%fused_computation.15 | loop fusion | flops 1310720 | bytes 5242880 | tf_op jit(solution)/shard_map/sub | solution.py:53
  125.9 2.7 copy.39
  128.6 2.8 copy.40
  131.5 18.6 %fusion.6 = (f32[1,32,64,128]{1,3,2,0:T(8,128)}, f32[1,32,64,128]{1,3,2,0:T(8,128)}) fusion(f32[3,34,66,128]{1,3,2,0:T(8,128)} %copy.23, f32[3,34,66,1]{1,3,2,0:T(1,128)} %collective-permute-done.5, f32[3,34,66,1]{1,3,2,0:T(1,128)} %collective-permute-done.4, f32[1,32,64,128]{1,3,2,0:T(8,128)} %copy.39, f32[1,32,64,128]{1,3,2,0:T(8,128)} %copy.40, ...), kind=kLoop, calls=%fused_computation.14 | loop fusion | flops 3670016 | bytes 9792096 | tf_op jit(solution)/shard_map/sub | solution.py:51
  150.0 10.3 %maximum_bitcast_fusion = f32[3,32,8,8,8,16]{1,5,3,4,2,0:T(8,128)} fusion(f32[1,32,8,8,8,16]{1,5,4,3,2,0:T(8,128)S(1)} %bitcast.66, f32[1,32,8,8,8,16]{1,5,4,3,2,0:T(8,128)} %bitcast.68, f32[1,32,8,8,8,16]{1,5,4,3,2,0:T(8,128)} %bitcast.67), kind=kLoop, calls=%fused_computation.3 | loop fusion | flops 1572864 | bytes 6291456 | tf_op jit(solution)/shard_map/dot_general | solution.py:61
  160.3 23.0 %copy.47 = f32[3,32,8,8,8,16]{5,3,2,1,4,0:T(8,128)} copy(f32[3,32,8,8,8,16]{1,5,3,4,2,0:T(8,128)} %maximum_bitcast_fusion) | data formatting | bytes 6291456 | tf_op jit(solution)/shard_map/dot_general | solution.py:61
  183.4 24.2 %multiply_reduce_fusion = (f32[]{:T(128)}, f32[3,2048,128]{2,1,0:T(8,128)S(1)}) fusion(f32[3,2048,8,16]{3,1,2,0:T(8,128)} %bitcast.63, f32[8,16,128,1]{2,1,0,3:T(8,128)S(1)} %bitcast.70), kind=kOutput, calls=%fused_computation.17 | convolution fusion | flops 1209532416 | bytes 6356996 | tf_op jit(solution)/shard_map/dot_general | solution.py:61
  207.6 1.4 dynamic-update-slice
  209.6 7.4 %all-reduce = f32[4]{0:T(128)S(1)} all-reduce(f32[4]{0:T(128)S(1)} %dynamic-update-slice), channel_id=1, replica_groups=mesh['gx_0'=4,'gx_1'=2,'gy'=8,'wa'=4] {'gx_0'}, use_global_device_ids=true, to_apply=%add | all-reduce | flops 4 | bytes 32
  217.6 1.4 dynamic-update-slice.1
  219.2 6.3 %all-reduce.1 = f32[2]{0:T(128)S(1)} all-reduce(f32[2]{0:T(128)S(1)} %dynamic-update-slice.1), channel_id=1, replica_groups=mesh['gx_0'=4,'gx_1'=2,'gy'=8,'wa'=4] {'gx_1'}, use_global_device_ids=true, to_apply=%add.1 | all-reduce | flops 2 | bytes 16
  226.1 1.3 dynamic-update-slice.2
  227.4 10.0 %copy.34 = f32[3,2048,128]{2,0,1:T(4,128)} copy(f32[3,2048,128]{2,1,0:T(8,128)S(1)} %get-tuple-element.33) | data formatting | bytes 6291456 | tf_op jit(solution)/shard_map/dot_general | solution.py:61
  237.4 13.6 %all-reduce.2 = f32[8]{0:T(128)S(1)} all-reduce(f32[8]{0:T(128)S(1)} %dynamic-update-slice.2), channel_id=1, replica_groups=mesh['gx_0'=4,'gx_1'=2,'gy'=8,'wa'=4] {'gy'}, use_global_device_ids=true, to_apply=%add.2 | all-reduce | flops 8 | bytes 64
  251.0 0.7 reduce_sum.61
  251.7 1.4 dynamic-update-slice.3
  253.1 32.5 %gather_fusion.1 = f32[4096,3,128]{2,1,0:T(4,128)} fusion(f32[3,2048,128]{2,0,1:T(4,128)} %copy.34, s32[4096]{0:T(1024)S(1)} %maximum_clamp_fusion), kind=kCustom, calls=%fused_computation.1 | custom fusion | bytes 12599296 | tf_op jit(solution)/shard_map/jit(_take)/gather | solution.py:95
  285.6 9.1 %all-reduce.3 = f32[4]{0:T(128)S(1)} all-reduce(f32[4]{0:T(128)S(1)} %dynamic-update-slice.3), channel_id=1, replica_groups=mesh['gx_0'=4,'gx_1'=2,'gy'=8,'wa'=4] {'wa'}, use_global_device_ids=true, to_apply=%add.3 | all-reduce | flops 4 | bytes 32
  296.0 5.0 %fusion.1 = f32[3,64,64,128]{3,2,0,1:T(8,128)S(1)} fusion(f32[3,64,64,128]{3,0,2,1:T(4,128)} %bitcast.64, f32[]{:T(128)S(6)} %sqrt.3, pred[64,64]{1,0:T(8,128)(4,1)S(1)} %broadcast_in_dim.69, pred[64,64,128]{2,1,0:T(8,128)(4,1)S(1)} %copy-done.6), kind=kLoop, calls=%fused_computation.6 | loop fusion | flops 4718592 | bytes 13111300 | tf_op jit(solution)/shard_map/jit(_where)/select_n | solution.py:98
  301.0 151.2 %all_to_all.5 = f32[3,64,64,128]{3,2,0,1:T(8,128)S(1)} all-to-all(f32[3,64,64,128]{3,2,0,1:T(8,128)S(1)} %fusion.1), channel_id=1, replica_groups=mesh['gx_0'=4,'gx_1'=2,'gy'=8,'wa'=4] {'gx_0','gx_1','gy'}, dimensions={1} | all-to-all | bytes 12582912 | tf_op jit(solution)/shard_map/all_to_all | solution.py:100
  452.3 3.3 copy.36
  (63 shorter events, 6.3 us)
Async XLA Ops:
  0.0 32.6 %copy-start = (s32[1,1,1,2048]{3,2,1,0:T(1,128)S(1)}, s32[1,1,1,2048]{3,2,1,0:T(1,128)}, u32[]{:S(2)}) copy-start(s32[1,1,1,2048]{3,2,1,0:T(1,128)} %param.4) | copy-start | bytes 24580
  0.0 24.2 %copy-start.7 = (s32[1,1,1,2048,1]{3,4,2,1,0:T(1,128)S(1)}, s32[1,1,1,2048,1]{3,4,2,1,0:T(1,128)}, u32[]{:S(2)}) copy-start(s32[1,1,1,2048,1]{3,4,2,1,0:T(1,128)} %param.5) | copy-start | bytes 24580
  1.0 59.7 %collective-permute-start = (f32[3,1,64,128]{3,2,1,0:T(8,128)S(1)}, f32[3,1,64,128]{3,2,1,0:T(8,128)}, u32[]{:S(2)}, u32[]{:S(2)}) collective-permute-start(f32[3,1,64,128]{3,2,1,0:T(8,128)S(1)} %get-tuple-element.27), channel_id=1, source_target_pairs={{0,32},{32,64},{64,96},{96,128},{128,160},{160,192},{192,224},{224... | collective-permute-start | bytes 294920 | tf_op jit(solution)/shard_map/ppermute | solution.py:21
  3.6 60.8 %collective-permute-start.1 = (f32[3,1,64,128]{3,2,1,0:T(8,128)S(1)}, f32[3,1,64,128]{3,2,1,0:T(8,128)}, u32[]{:S(2)}, u32[]{:S(2)}) collective-permute-start(f32[3,1,64,128]{3,2,1,0:T(8,128)S(1)} %get-tuple-element.26), channel_id=1, source_target_pairs={{32,0},{64,32},{96,64},{128,96},{160,128},{192,160},{224,192},{0,2... | collective-permute-start | bytes 294920 | tf_op jit(solution)/shard_map/ppermute | solution.py:22
  32.6 26.2 %copy-start.11 = (u32[256]{0:T(256)S(1)}, u32[256]{0:T(256)}, u32[]{:S(2)}) copy-start(u32[256]{0:T(256)} %constant.77) | copy-start | bytes 3076
  32.6 26.8 %copy-start.10 = (u32[256]{0:T(256)S(1)}, u32[256]{0:T(256)}, u32[]{:S(2)}) copy-start(u32[256]{0:T(256)} %constant.82) | copy-start | bytes 3076
  32.6 27.5 %copy-start.9 = (u32[256]{0:T(256)S(1)}, u32[256]{0:T(256)}, u32[]{:S(2)}) copy-start(u32[256]{0:T(256)} %constant.87) | copy-start | bytes 3076
  66.0 22.8 %collective-permute-start.2 = (f32[3,34,1,128]{3,2,1,0:T(1,128)}, f32[3,34,1,128]{3,2,1,0:T(1,128)S(1)}, u32[]{:S(2)}, u32[]{:S(2)}) collective-permute-start(f32[3,34,1,128]{3,2,1,0:T(1,128)} %get-tuple-element.18), channel_id=1, source_target_pairs={{4,0},{8,4},{12,8},{16,12},{20,16},{24,20},{28,24},{0,28},{5,1},{9... | collective-permute-start | bytes 156680 | tf_op jit(solution)/shard_map/ppermute | solution.py:22
  71.0 17.8 %collective-permute-start.3 = (f32[3,34,1,128]{3,2,1,0:T(1,128)}, f32[3,34,1,128]{3,2,1,0:T(1,128)S(1)}, u32[]{:S(2)}, u32[]{:S(2)}) collective-permute-start(f32[3,34,1,128]{3,2,1,0:T(1,128)} %get-tuple-element.17), channel_id=1, source_target_pairs={{0,4},{4,8},{8,12},{12,16},{16,20},{20,24},{24,28},{28,0},{1,5},{5... | collective-permute-start | bytes 156680 | tf_op jit(solution)/shard_map/ppermute | solution.py:21
  103.7 27.8 %collective-permute-start.4 = (f32[3,34,66,1]{1,3,2,0:T(1,128)}, f32[3,34,66,1]{1,3,2,0:T(1,128)}, u32[]{:S(2)}, u32[]{:S(2)}) collective-permute-start(f32[3,34,66,1]{1,3,2,0:T(1,128)} %get-tuple-element.9), channel_id=1, source_target_pairs={{1,0},{2,1},{3,2},{0,3},{5,4},{6,5},{7,6},{4,7},{9,8},{10,9},{11,1... | collective-permute-start | bytes 80792 | tf_op jit(solution)/shard_map/ppermute | solution.py:22
  106.4 25.0 %collective-permute-start.5 = (f32[3,34,66,1]{1,3,2,0:T(1,128)}, f32[3,34,66,1]{1,3,2,0:T(1,128)}, u32[]{:S(2)}, u32[]{:S(2)}) collective-permute-start(f32[3,34,66,1]{1,3,2,0:T(1,128)} %get-tuple-element.10), channel_id=1, source_target_pairs={{0,1},{1,2},{2,3},{3,0},{4,5},{5,6},{6,7},{7,4},{8,9},{9,10},{10,1... | collective-permute-start | bytes 80792 | tf_op jit(solution)/shard_map/ppermute | solution.py:21
  109.1 3.8 copy-start.5
  115.6 10.3 %copy-start.4 = (f32[1,32,64,128]{3,2,1,0:T(8,128)S(1)}, f32[1,32,64,128]{3,2,1,0:T(8,128)}, u32[]{:S(2)}) copy-start(f32[1,32,64,128]{3,2,1,0:T(8,128)} %get-tuple-element.16) | copy-start | bytes 3145732
  125.9 2.7 copy-start.3
  131.4 18.6 %copy-start.2 = (f32[1,32,64,128]{1,3,2,0:T(8,128)S(1)}, f32[1,32,64,128]{1,3,2,0:T(8,128)}, u32[]{:S(2)}) copy-start(f32[1,32,64,128]{1,3,2,0:T(8,128)} %multiply_subtract_fusion) | copy-start | bytes 3145732
  183.4 25.6 %copy-start.8 = (u32[256]{0:T(256)S(1)}, u32[256]{0:T(256)}, u32[]{:S(2)}) copy-start(u32[256]{0:T(256)} %constant.92) | copy-start | bytes 3076
  253.1 42.9 %copy-start.6 = (pred[64,64,128]{2,1,0:T(8,128)(4,1)S(1)}, pred[64,64,128]{2,1,0:T(8,128)(4,1)}, u32[]{:S(2)}) copy-start(pred[64,64,128]{2,1,0:T(8,128)(4,1)} %fusion.7) | copy-start | bytes 1572868
  452.3 3.3 copy-start.1
